TPU v7x, 32 devices: a whole 2x2x4 slice. The times are simulated.
32 devices in a mesh: dp: 4 (over x, y), tp: 8 (over z, core).
Axes of the slice: x: 2, y: 2, z: 4, core: 2. Of those that a mesh axis runs over, the one named last changes fastest.
Arguments:
- x: bfloat16 [5120, 7168], P(('dp', 'tp')), parts along dimension 0
- w_gate: bfloat16 [7168, 20480], P(None, 'tp')
- w_up: bfloat16 [7168, 20480], P(None, 'tp')
- w_down: bfloat16 [20480, 7168], P('tp')
Outputs:
- output: bfloat16 [5120, 7168], P(('dp', 'tp')), parts along dimension 0
There are 4 independent parts. A program takes and returns all parts, laid end to end along the dimension named above; an argument that names none is the same for every part.
All inputs are finite; a program needn't handle non-finite values.
Results may differ from a plain program's by a relative error of at most 0.016.
Values are sent between devices in bfloat16 or wider.
A program may use at most 2 GiB of HBM per device.

v0:
```python
import jax
import jax.numpy as jnp
from jax import lax
from jax.sharding import PartitionSpec as P


def solution(mesh):
    def step(x, w_gate, w_up, w_down):
        rows = lax.all_gather(x, "tp", axis=0, tiled=True)
        gate = jnp.dot(rows, w_gate, preferred_element_type=jnp.float32)
        up = jnp.dot(rows, w_up, preferred_element_type=jnp.float32)
        hidden = (jax.nn.silu(gate) * up).astype(jnp.bfloat16)
        term = jnp.dot(hidden, w_down, preferred_element_type=jnp.float32).astype(jnp.bfloat16)
        return lax.psum_scatter(term, "tp", scatter_dimension=0, tiled=True)

    return jax.shard_map(
        step,
        mesh=mesh,
        in_specs=(P(("dp", "tp"), None), P(None, "tp"), P(None, "tp"), P("tp", None)),
        out_specs=P(("dp", "tp"), None),
        check_vma=False,
    )
```

profile of v0, /device:TPU:0, one launch (start us, length us, event | category | flops | bytes accessed | tf_op | source)
XLA Modules:
  0.0 535.2 jit_solution(1292684379234210434)
XLA Ops:
  6.5 0.0 all-gather.2.cloned.1.call-start
  6.5 0.7 all-gather.2.cloned.1.call-update
  7.3 0.0 reduce-scatter.2.cloned.1.call-start
  7.3 168.4 %all-gather.2.cloned.1.call-done = bf16[1280,7168]{1,0:T(8,128)(2,1)} async-done(((bf16[160,7168]{1,0:T(8,128)(2,1)}), bf16[1280,7168]{1,0:T(8,128)(2,1)}) %all-gather.2.cloned.1.call-update) | async-done | bytes 18350096 | tf_op jit(solution)/shard_map/all_gather | solution.py:9
  175.8 58.6 %fusion.1 = f32[1280,2560]{1,0:T(8,128)} fusion(bf16[1280,7168]{1,0:T(8,128)(2,1)} %all-gather.2.cloned.1.call-done, bf16[7168,2560]{1,0:T(8,128)(2,1)} %param.5), kind=kOutput, calls=%fused_computation.3 | convolution fusion | flops 46976204800 | bytes 68157440 | tf_op jit(solution)/shard_map/dot_general | solution.py:10
  234.3 59.5 %fusion = bf16[1280,2560]{1,0:T(8,128)(2,1)S(1)} fusion(bf16[1280,7168]{1,0:T(8,128)(2,1)} %all-gather.2.cloned.1.call-done, bf16[7168,2560]{1,0:T(8,128)(2,1)} %param.6, f32[1280,2560]{1,0:T(8,128)} %fusion.1), kind=kOutput, calls=%fused_computation.2 | convolution fusion | flops 46995865600 | bytes 74711040 | tf_op jit(solution)/shard_map/dot_general | solution.py:11
  293.8 52.8 %convolution_convert_fusion = bf16[1280,7168]{1,0:T(8,128)(2,1)} fusion(bf16[1280,2560]{1,0:T(8,128)(2,1)S(1)} %fusion, bf16[2560,7168]{1,0:T(8,128)(2,1)} %param.7), kind=kOutput, calls=%fused_computation | convolution fusion | flops 46985379840 | bytes 61603840 | tf_op jit(solution)/shard_map/dot_general | solution.py:13
  346.6 0.0 reduce-scatter.2.cloned.1.call-update
  346.7 181.7 %reduce-scatter.2.cloned.1.call-done = bf16[160,7168]{1,0:T(8,128)(2,1)} async-done(((bf16[1280,7168]{1,0:T(8,128)(2,1)}), bf16[160,7168]{1,0:T(8,128)(2,1)}) %reduce-scatter.2.cloned.1.call-update) | async-done | bytes 2293776 | tf_op jit(solution)/shard_map/reduce_scatter | solution.py:14
Async XLA Ops:
  6.5 169.2 %all-gather.2.cloned.1.call-start = ((), (), s32[]{:S(2)}) async-start(), calls=%async_computation.1 | async-start | bytes 20643840 | tf_op jit(solution)/shard_map/all_gather | solution.py:9
  7.3 521.1 %reduce-scatter.2.cloned.1.call-start = ((), (), s32[]{:S(2)}) async-start(), calls=%async_computation.2 | async-start | bytes 20643840 | tf_op jit(solution)/shard_map/reduce_scatter | solution.py:14
Sparse Core Ops, SparseCore 0:
  9.0 166.7 all-gather.1
  346.8 181.5 reduce-scatter.1
where the time goes:
time: 535 us
  waiting for transfers between devices  351 us (66%)
  matrix products  171 us (32%)
  between operations  13.4 us (3%)
    reduce_scatter x1, waiting for transfers between devices, step(): return lax.psum_scatter(term, 'tp', scatter_dimension=0, tiled=True)  182 us
    all_gather x1, waiting for transfers between devices, step(): rows = lax.all_gather(x, 'tp', axis=0, tiled=True)  168 us
    dot_general x1, matrix products, step(): up = jnp.dot(rows, w_up, preferred_element_type=jnp.float32)  59.5 us
    dot_general x1, matrix products, step(): gate = jnp.dot(rows, w_gate, preferred_element_type=jnp.float32)  58.6 us
    dot_general x1, matrix products, step(): jnp.dot(hidden, w_down, preferred_element_type=jnp.float32)  52.8 us
  transfers between devices with their start and end apart: 2, of which 2 were waited for; matrix products, arithmetic and copies ran while one was open for 0% of the time, Pallas kernels for 0%

commit v1 on v0

v1 whole, which is shorter than its diff:
```python
import jax
import jax.numpy as jnp
from jax import lax
from jax.experimental import pallas as pl
from jax.experimental.pallas import tpu as pltpu
from jax.sharding import PartitionSpec as P

MESH = pl.DeviceIdType.MESH
F32, BF16 = jnp.float32, jnp.bfloat16

D = 7168
F = 2560
R = 160
NP, RP = 5, 32
KH = D // 2
GW, NG = 256, F // 256
DW, ND = 512, D // 512
TOT = 2 * NG + ND
NS = 4
PS = 4
LAG = 3


def kernel(x_ref, wg_ref, wu_ref, wd_ref, y_ref, xg, xb, ring, hid, acc, stash, pst, pt, rs,
           wsem, xsem, ag_recv, agp_recv, fwd_send, out_send, d2d_send,
           pst_send, pt_recv, rs_send, rs_recv, ysem):
    tp = lax.axis_index("tp")
    z, c = tp // 2, tp % 2
    mir = z // 2
    mid = (z * (3 - z)) // 2
    is_mid, is_end = mid == 1, mid == 0
    din = 1 - 2 * mir
    partner = {"tp": 2 * z + (1 - c)}
    inward = {"tp": 2 * (z + din) + c}
    outward = {"tp": 2 * (z - din * mid) + c}

    def real(bb):
        return bb + mir * (3 - 2 * bb)

    def block(s):
        m = ((s + 1) % 3) * (1 - s // 3) + 3 * (s // 3)
        return mid * m + (1 - mid) * s

    barrier = pltpu.get_barrier_semaphore()
    pl.semaphore_signal(barrier, inc=1, device_id=partner, device_id_type=MESH)
    pl.semaphore_signal(barrier, inc=1, device_id=inward, device_id_type=MESH)

    @pl.when(is_mid)
    def _():
        pl.semaphore_signal(barrier, inc=1, device_id=outward, device_id_type=MESH)

    def gu_copy(ref, i, kh, slot, h):
        return pltpu.make_async_copy(
            ref.at[pl.ds(pl.multiple_of(kh * KH, KH), KH), pl.ds(pl.multiple_of(i * GW, GW), GW)],
            ring.at[slot, :, pl.ds(h * GW, GW)], wsem.at[slot, h])

    def d_copy(j, slot):
        return pltpu.make_async_copy(
            wd_ref.at[:, pl.ds(pl.multiple_of(j * DW, DW), DW)],
            ring.at[slot, pl.ds(0, F)], wsem.at[slot, 0])

    def fetch(g):
        q, slot = lax.rem(g, TOT), lax.rem(g, NS)

        @pl.when((g < 4 * TOT) & (q < 2 * NG))
        def _():
            gu_copy(wg_ref, q // 2, q % 2, slot, 0).start()
            gu_copy(wu_ref, q // 2, q % 2, slot, 1).start()

        @pl.when((g < 4 * TOT) & (q >= 2 * NG))
        def _():
            d_copy(q - 2 * NG, slot).start()

    for k in range(NS - 1):
        fetch(jnp.int32(k))

    def rows(p):
        return pl.ds(pl.multiple_of(p * RP, RP), RP)

    def send_x(src, b, p, sem, recv, dev):
        return pltpu.make_async_remote_copy(
            src_ref=src.at[rows(p)], dst_ref=xg.at[b, c, rows(p)], send_sem=sem.at[b, p],
            recv_sem=recv.at[b, p], device_id=dev, device_id_type=MESH)

    def own_x(p, kind):
        if kind == 0:
            return send_x(x_ref, z, p, d2d_send, agp_recv, partner)
        if kind == 1:
            return send_x(x_ref, z, p, fwd_send, ag_recv, inward)
        return send_x(x_ref, z, p, out_send, ag_recv, outward)

    def arrived(b, p):
        send_x(xg.at[b, c], b, p, fwd_send, ag_recv, partner).wait_recv()

    def forward(b, p, dev):
        return send_x(xg.at[b, c], b, p, fwd_send, ag_recv, dev)

    def share(b, p):
        return send_x(xg.at[b, c], b, p, d2d_send, agp_recv, partner)

    def relay(s, p):
        @pl.when(is_end & (s < 3))
        def _():
            b = real(s + 1)
            arrived(b, p)
            share(b, p).start()

        @pl.when(is_mid & (s == 0))
        def _():
            b0, b2 = real(0), real(2)
            arrived(b2, p)
            forward(b2, p, outward).start()
            share(b2, p).start()
            arrived(b0, p)
            forward(b0, p, inward).start()
            share(b0, p).start()

        @pl.when(is_mid & (s == 1))
        def _():
            b3 = real(3)
            arrived(b3, p)
            forward(b3, p, outward).start()
            share(b3, p).start()

    def x_load_own(b):
        return pltpu.make_async_copy(xg.at[b, c], xb.at[pl.ds(0, R)], xsem.at[0])

    def x_load_partner(b):
        return pltpu.make_async_copy(xg.at[b, 1 - c], xb.at[pl.ds(R, R)], xsem.at[1])

    def wait_partner_x(b):
        @pl.loop(0, NP)
        def _(p):
            pltpu.make_async_remote_copy(
                src_ref=xg.at[b, 1 - c, rows(p)], dst_ref=xg.at[b, 1 - c, rows(p)],
                send_sem=d2d_send.at[b, p], recv_sem=agp_recv.at[b, p],
                device_id=partner, device_id_type=MESH).wait_recv()

    def send_pt(s, j):
        return pltpu.make_async_remote_copy(
            src_ref=pst.at[j % PS], dst_ref=pt.at[s % 2, j], send_sem=pst_send.at[j % PS],
            recv_sem=pt_recv.at[s % 2, j], device_id=partner, device_id_type=MESH)

    def send_rs(slot, there, j, dev):
        return pltpu.make_async_remote_copy(
            src_ref=rs.at[slot, j], dst_ref=rs.at[there, j], send_sem=rs_send.at[slot, j],
            recv_sem=rs_recv.at[there, j], device_id=dev, device_id_type=MESH)

    def rs_arrived(slot, j):
        send_rs(0, slot, j, inward).wait_recv()

    def fold(s, k):
        send_pt(s, k).wait_recv()
        v = stash[s, k] + pt[s % 2, k].astype(F32)

        @pl.when(is_end & (s >= 1))
        def _():
            rs[s, k] = v.astype(BF16)

        @pl.when(is_mid | (s == 0))
        def _():
            stash[s, k] = v

    def end_send(s, k):
        @pl.when(is_end & (s >= 1))
        def _():
            send_rs(s, s, k, inward).start()

    def add_in(slot, s, k):
        rs_arrived(slot, k)
        rs[slot, k] = (stash[s, k] + rs[slot, k].astype(F32)).astype(BF16)

    def second(k):
        @pl.when(k >= 1)
        def _():
            send_rs(2, 4, k - 1, inward).start()

        add_in(2, 1, k)

    x_own = pltpu.make_async_copy(x_ref, xb.at[pl.ds(0, R)], xsem.at[0])
    x_own.start()
    pl.semaphore_wait(barrier, 2 + mid)

    @pl.loop(0, NP)
    def _(p):
        own_x(p, 0).start()
        own_x(p, 1).start()

        @pl.when(is_mid)
        def _():
            own_x(p, 2).start()

    wait_partner_x(z)
    x_load_partner(z).start()
    x_own.wait()
    x_load_partner(z).wait()

    @pl.loop(0, 4)
    def _(s):
        base = s * TOT

        @pl.loop(0, NG)
        def _(i):
            g = base + 2 * i
            s0, s1 = lax.rem(g, NS), lax.rem(g + 1, NS)
            fetch(g + NS - 1)
            gu_copy(wg_ref, i, 0, s0, 0).wait()
            gu_copy(wu_ref, i, 0, s0, 1).wait()
            acc[...] = jnp.dot(xb[:, :KH], ring[s0], preferred_element_type=F32)
            fetch(g + NS)
            gu_copy(wg_ref, i, 1, s1, 0).wait()
            gu_copy(wu_ref, i, 1, s1, 1).wait()
            t = acc[...] + jnp.dot(xb[:, KH:], ring[s1], preferred_element_type=F32)
            hid[:, pl.ds(pl.multiple_of(i * GW, GW), GW)] = (
                jax.nn.silu(t[:, :GW]) * t[:, GW:]).astype(BF16)

            @pl.when((i == 3) | (i == 6))
            def _():
                relay(s, i // 3 - 1)

            @pl.when(is_mid & (s == 2) & (i == 3))
            def _():
                relay(jnp.int32(1), jnp.int32(4))

            @pl.when(is_mid & (s == 3) & (i >= 2))
            def _():
                second(i - 2)

        early = is_mid & ((s == 1) | (s == 2))
        nxt = real(block(s + 1))

        @pl.when(early)
        def _():
            wait_partner_x(nxt)
            x_load_own(nxt).start()
            x_load_partner(nxt).start()

        @pl.loop(0, ND)
        def _(j):
            g = base + 2 * NG + j
            s0 = lax.rem(g, NS)
            fetch(g + NS - 1)
            d_copy(j, s0).wait()
            t = jnp.dot(hid[...], ring[s0, :F], preferred_element_type=F32)

            @pl.when(j >= PS)
            def _():
                send_pt(s, j - PS).wait_send()

            stash[s, j] = t[:R]
            pst[j % PS] = t[R:].astype(BF16)

            @pl.when(j >= 1)
            def _():
                send_pt(s, j - 1).start()

            @pl.when(j >= LAG + 1)
            def _():
                end_send(s, j - LAG - 1)

            @pl.when(j >= LAG)
            def _():
                fold(s, j - LAG)

            @pl.when((j == 2) | (j == 11))
            def _():
                relay(s, 2 + j // 11)

            @pl.when(is_mid & (s == 3) & (j >= 2) & (j % 2 == 0))
            def _():
                second(NG - 2 + j // 2 - 1)

        send_pt(s, ND - 1).start()
        end_send(s, ND - LAG - 1)

        @pl.when(is_end | (s == 0))
        def _():
            relay(s, jnp.int32(4))

        @pl.when((s < 3) & jnp.logical_not(early))
        def _():
            x_load_own(nxt).start()

        @pl.loop(ND - LAG, ND)
        def _(k):
            fold(s, k)

        @pl.when((s < 3) & jnp.logical_not(early))
        def _():
            wait_partner_x(nxt)
            x_load_partner(nxt).start()

        @pl.loop(ND - LAG, ND)
        def _(k):
            end_send(s, k)

        @pl.loop(ND - PS, ND)
        def _(k):
            send_pt(s, k).wait_send()

        @pl.when(s < 3)
        def _():
            x_load_own(nxt).wait()
            x_load_partner(nxt).wait()

    def y_copy(slot, k):
        return pltpu.make_async_copy(
            rs.at[slot, k], y_ref.at[:, pl.ds(pl.multiple_of(k * DW, DW), DW)], ysem.at[k])

    @pl.when(is_mid)
    def _():
        send_rs(2, 4, ND - 1, inward).start()

        @pl.loop(0, ND + 1)
        def _(k):
            @pl.when(k < ND)
            def _():
                add_in(3, 3, k)
                rs_arrived(1, k)
                rs_arrived(4, k)
                rs[1, k] = (stash[0, k] + rs[1, k].astype(F32) + rs[4, k].astype(F32)).astype(BF16)
                send_rs(3, 0, k, inward).start()

            @pl.when(k >= 1)
            def _():
                y_copy(1, k - 1).start()
                add_in(0, 2, k - 1)

            @pl.when(k >= 2)
            def _():
                send_rs(0, 0, k - 2, outward).start()

        send_rs(0, 0, ND - 1, outward).start()

        @pl.loop(0, ND)
        def _(k):
            y_copy(1, k).wait()
            send_rs(2, 4, k, inward).wait_send()
            send_rs(3, 0, k, inward).wait_send()
            send_rs(0, 0, k, outward).wait_send()

    @pl.when(is_end)
    def _():
        @pl.loop(0, ND)
        def _(k):
            add_in(0, 0, k)

            @pl.when(k >= 1)
            def _():
                y_copy(0, k - 1).start()

        y_copy(0, ND - 1).start()

        @pl.loop(0, ND)
        def _(k):
            y_copy(0, k).wait()
            for s in (1, 2, 3):
                send_rs(s, s, k, inward).wait_send()

    @pl.loop(0, NP)
    def _(p):
        own_x(p, 0).wait_send()
        own_x(p, 1).wait_send()

        @pl.when(is_mid)
        def _():
            own_x(p, 2).wait_send()
            for bb in (0, 2, 3):
                forward(real(bb), p, inward).wait_send()
                share(real(bb), p).wait_send()

        @pl.when(is_end)
        def _():
            for bb in (1, 2, 3):
                share(real(bb), p).wait_send()


def solution(mesh):
    dma = pltpu.SemaphoreType.DMA

    def step(x, w_gate, w_up, w_down):
        hbm = pl.BlockSpec(memory_space=pltpu.HBM)
        y, _ = pl.pallas_call(
            kernel,
            name="mlp",
            out_shape=(jax.ShapeDtypeStruct((R, D), BF16),
                       jax.ShapeDtypeStruct((4, 2, R, D), BF16)),
            in_specs=[hbm] * 4,
            out_specs=(hbm, hbm),
            scratch_shapes=[
                pltpu.VMEM((2 * R, D), BF16),
                pltpu.VMEM((NS, KH, DW), BF16),
                pltpu.VMEM((2 * R, F), BF16),
                pltpu.VMEM((2 * R, 2 * GW), F32),
                pltpu.VMEM((4, ND, R, DW), F32),
                pltpu.VMEM((PS, R, DW), BF16),
                pltpu.VMEM((2, ND, R, DW), BF16),
                pltpu.VMEM((5, ND, R, DW), BF16),
                dma((NS, 2)), dma((2,)),
                dma((4, NP)), dma((4, NP)), dma((4, NP)), dma((4, NP)), dma((4, NP)),
                dma((PS,)), dma((2, ND)), dma((4, ND)), dma((5, ND)), dma((ND,)),
            ],
            compiler_params=pltpu.CompilerParams(
                collective_id=0, has_side_effects=True, vmem_limit_bytes=67043328),
        )(x, w_gate, w_up, w_down)
        return y

    return jax.shard_map(
        step,
        mesh=mesh,
        in_specs=(P(("dp", "tp"), None), P(None, "tp"), P(None, "tp"), P("tp", None)),
        out_specs=P(("dp", "tp"), None),
        check_vma=False,
    )
```

time: 535 us -> 275 us (0.51)
  waiting for transfers between devices: 351 us -> 0 us
  Pallas kernels: 0 us -> 272 us
  matrix products: 171 us -> 0 us
  between operations: 13.4 us -> 0.01 us
    pallas_call x0 -> x1, Pallas kernels: none -> 272 us  [step(): pl.pallas_call(kernel, name='mlp', out_shape=(jax.ShapeDtypeStruct((R, D)...]
    reduce_scatter x1 -> x0, waiting for transfers between devices: 182 us -> none  [step(): return lax.psum_scatter(term, 'tp', scatter_dimension=0, tiled=True)]
    dot_general x3 -> x0, matrix products: 171 us -> none  [the longest x1 59.5 us: step(): up = jnp.dot(rows, w_up, preferred_element_type=jnp.float32)]
    all_gather x1 -> x0, waiting for transfers between devices: 168 us -> none  [step(): rows = lax.all_gather(x, 'tp', axis=0, tiled=True)]
  transfers between devices with their start and end apart: 2 -> 0, of which waited for: 2 -> 0; matrix products, arithmetic and copies ran while one was open for 0% -> 0% of each run, Pallas kernels for 0% -> 0%
where the time goes in v1:
time: 275 us
  Pallas kernels  272 us (99%)
  local copies, waits for them, and re-layouts  3.18 us (1%)
    pallas_call x1, Pallas kernels, step(): pl.pallas_call(kernel, name='mlp', out_shape=(jax.ShapeDtypeStruct((R, D)...  272 us

profile of v1, /device:TPU:0, one launch (start us, length us, event | category | flops | bytes accessed | tf_op | source)
XLA Modules:
  0.0 275.0 jit_solution(4422572207014787408)
XLA Ops:
  0.0 271.9 %mlp.1 = (bf16[160,7168]{1,0:T(8,128)(2,1)}, bf16[4,2,160,7168]{3,2,1,0:T(8,128)(2,1)}) custom-call(bf16[160,7168]{1,0:T(8,128)(2,1)} %x_ref.1, bf16[7168,2560]{1,0:T(8,128)(2,1)} %wg_ref.1, bf16[7168,2560]{1,0:T(8,128)(2,1)} %wu_ref.1, bf16[2560,7168]{1,0:T(8,128)(2,1)} %wd_ref.1), custom_call_target="tpu_custom_call" | custom-call | tf_op jit(solution)/shard_map/mlp/pallas_call | solution.py:383
  271.9 3.2 %copy.6 = bf16[160,7168]{1,0:T(8,128)(2,1)} copy(bf16[160,7168]{1,0:T(8,128)(2,1)} %get-tuple-element.6) | data formatting | bytes 4587520

commit v2 on v0

v2 whole, which is shorter than its diff:
```python
import jax
import jax.numpy as jnp
from jax import lax
from jax.experimental import pallas as pl
from jax.experimental.pallas import tpu as pltpu
from jax.sharding import PartitionSpec as P

MESH = pl.DeviceIdType.MESH
F32, BF16 = jnp.float32, jnp.bfloat16

D = 7168
F = 2560
R = 160
NP = 4
KC = D // NP
GW, NG = 512, F // 512
DW, ND = 512, D // 512
ND2, FH = ND // 2, F // 2
GU = NP * NG
TOT = GU + ND
NS = 5
PS = 4


def kernel(x_ref, wg_ref, wu_ref, wd_ref, y_ref, xg, xb, ring, hid, acc, stash, pst, pt, rs,
           wsem, xsem, ag_recv, agp_recv, fwd_send, out_send, d2d_send,
           pst_send, pt_recv, rs_send, rs_recv, ysem):
    tp = lax.axis_index("tp")
    z, c = tp // 2, tp % 2
    mir = z // 2
    mid = (z * (3 - z)) // 2
    is_mid, is_end = mid == 1, mid == 0
    din = 1 - 2 * mir
    partner = {"tp": 2 * z + (1 - c)}
    inward = {"tp": 2 * (z + din) + c}
    outward = {"tp": 2 * (z - din * mid) + c}

    def real(bb):
        return bb + mir * (3 - 2 * bb)

    def block(s):
        m = ((s + 1) % 3) * (1 - s // 3) + 3 * (s // 3)
        return mid * m + (1 - mid) * s

    barrier = pltpu.get_barrier_semaphore()
    pl.semaphore_signal(barrier, inc=1, device_id=partner, device_id_type=MESH)
    pl.semaphore_signal(barrier, inc=1, device_id=inward, device_id_type=MESH)

    @pl.when(is_mid)
    def _():
        pl.semaphore_signal(barrier, inc=1, device_id=outward, device_id_type=MESH)

    def gu_copy(ref, u, slot, h):
        return pltpu.make_async_copy(
            ref.at[pl.ds(pl.multiple_of((u // NG) * KC, KC), KC),
                   pl.ds(pl.multiple_of((u % NG) * GW, GW), GW)],
            ring.at[slot, :, pl.ds(h * GW, GW)], wsem.at[slot, h])

    def d_copy(j, slot):
        return pltpu.make_async_copy(
            wd_ref.at[pl.ds(pl.multiple_of((j % 2) * FH, FH), FH),
                      pl.ds(pl.multiple_of((j // 2) * 2 * DW, 2 * DW), 2 * DW)],
            ring.at[slot, pl.ds(0, FH)], wsem.at[slot, 0])

    def fetch(g):
        slot = lax.rem(g, NS)
        r = lax.rem(g + ND, TOT)
        last = GU + 3 * TOT

        def gate_up(u):
            gu_copy(wg_ref, u, slot, 0).start()
            gu_copy(wu_ref, u, slot, 1).start()

        @pl.when(g < GU)
        def _():
            gate_up(g)

        @pl.when((g >= GU) & (g < last) & (r < GU))
        def _():
            gate_up(r)

        @pl.when((g >= GU) & (g < last) & (r >= GU))
        def _():
            d_copy(r - GU, slot).start()

        @pl.when((g >= last) & (g < last + ND))
        def _():
            d_copy(r, slot).start()

    for k in range(NS - 1):
        fetch(jnp.int32(k))

    def send_x(src, b, p, sem, recv, dev):
        return pltpu.make_async_remote_copy(
            src_ref=src, dst_ref=xg.at[b, c, p], send_sem=sem.at[b, p],
            recv_sem=recv.at[b, p], device_id=dev, device_id_type=MESH)

    def own_cols(p):
        return x_ref.at[:, pl.ds(pl.multiple_of(p * KC, KC), KC)]

    def own_x(p, kind):
        if kind == 0:
            return send_x(own_cols(p), z, p, d2d_send, agp_recv, partner)
        if kind == 1:
            return send_x(own_cols(p), z, p, fwd_send, ag_recv, inward)
        return send_x(own_cols(p), z, p, out_send, ag_recv, outward)

    def arrived(b, p):
        with jax.named_scope("w_ag"):
            send_x(xg.at[b, c, p], b, p, fwd_send, ag_recv, partner).wait_recv()

    def forward(b, p, dev):
        return send_x(xg.at[b, c, p], b, p, fwd_send, ag_recv, dev)

    def share(b, p):
        return send_x(xg.at[b, c, p], b, p, d2d_send, agp_recv, partner)

    def load_own(b, p):
        return pltpu.make_async_copy(xg.at[b, c, p], xb.at[p, pl.ds(0, R)], xsem.at[0, p])

    def load_partner(b, p):
        return pltpu.make_async_copy(xg.at[b, 1 - c, p], xb.at[p, pl.ds(R, R)], xsem.at[1, p])

    def partner_piece(b, p):
        with jax.named_scope("w_px"):
            pltpu.make_async_remote_copy(
                src_ref=xg.at[b, 1 - c, p], dst_ref=xg.at[b, 1 - c, p],
                send_sem=d2d_send.at[b, p], recv_sem=agp_recv.at[b, p],
                device_id=partner, device_id_type=MESH).wait_recv()
        load_partner(b, p).start()

    def relay_first(p):
        b = real(1 + mid)
        arrived(b, p)

        @pl.when(is_mid)
        def _():
            forward(b, p, outward).start()

        share(b, p).start()
        load_own(b, p).start()

        @pl.when(is_mid)
        def _():
            b0 = real(0)
            arrived(b0, p)
            forward(b0, p, inward).start()
            share(b0, p).start()

    def partner_first(p):
        partner_piece(real(1 + mid), p)

    def relay_end(bb, p):
        @pl.when(is_end)
        def _():
            arrived(real(bb), p)
            share(real(bb), p).start()
            load_own(real(bb), p).start()

    def partner_end(bb, p):
        @pl.when(is_end)
        def _():
            partner_piece(real(bb), p)

    def relay_mid(p):
        @pl.when(is_mid)
        def _():
            arrived(real(3), p)
            forward(real(3), p, outward).start()
            share(real(3), p).start()

    def load_mid(bb):
        @pl.when(is_mid)
        def _():
            @pl.loop(0, NP)
            def _(p):
                load_own(real(bb), p).start()
                partner_piece(real(bb), p)

    def send_pt(s, j):
        k = (ND * (s - 1) + j) % PS
        return pltpu.make_async_remote_copy(
            src_ref=pst.at[k], dst_ref=pt.at[k], send_sem=pst_send.at[k],
            recv_sem=pt_recv.at[k], device_id=partner, device_id_type=MESH)

    def send_rs(slot, there, j, dev):
        return pltpu.make_async_remote_copy(
            src_ref=rs.at[slot, j], dst_ref=rs.at[there, j], send_sem=rs_send.at[slot, j],
            recv_sem=rs_recv.at[there, j], device_id=dev, device_id_type=MESH)

    def rs_arrived(slot, j):
        with jax.named_scope("w_rs"):
            send_rs(0, slot, j, inward).wait_recv()

    def fold(s, k):
        with jax.named_scope("w_pt"):
            send_pt(s, k).wait_recv()
        v = stash[s % 4, k] + pt[(ND * (s - 1) + k) % PS].astype(F32)

        @pl.when(is_end & (s < 4))
        def _():
            rs[s, k] = v.astype(BF16)

        @pl.when(is_mid | (s == 4))
        def _():
            stash[s % 4, k] = v

    def end_send(s, k):
        @pl.when(is_end & (s < 4))
        def _():
            send_rs(s, s, k, inward).start()

    def add_in(slot, s, k):
        rs_arrived(slot, k)
        rs[slot, k] = (stash[s, k] + rs[slot, k].astype(F32)).astype(BF16)

    def pass_on(k):
        @pl.when(k < ND)
        def _():
            send_rs(2, 4, k, inward).start()

        @pl.when(k >= ND)
        def _():
            send_rs(3, 0, k - ND, inward).start()

    def take(k):
        @pl.when(k < ND)
        def _():
            add_in(2, 1, k)

        @pl.when(k >= ND)
        def _():
            add_in(3, 3, k - ND)

    def x_own(p):
        return pltpu.make_async_copy(own_cols(p), xb.at[p, pl.ds(0, R)], xsem.at[0, p])

    for p in range(NP):
        x_own(p).start()
    with jax.named_scope("w_bar"):
        pl.semaphore_wait(barrier, 2 + mid)

    @pl.loop(0, NP)
    def _(p):
        own_x(p, 0).start()
        own_x(p, 1).start()

        @pl.when(is_mid)
        def _():
            own_x(p, 2).start()

    @pl.loop(0, NP)
    def _(p):
        partner_piece(z, p)

    @pl.loop(0, 5)
    def _(s):
        base = (GU + (s - 1) * TOT) * ((s + 3) // 4)

        @pl.when(s < 4)
        def _():
            @pl.loop(0, GU)
            def _(q):
                kc, n = q // NG, q % NG

                @pl.when(n == 0)
                def _():
                    with jax.named_scope("w_xl"):
                        load_own(z, kc).wait()
                        load_partner(z, kc).wait()

                g = base + q
                slot = lax.rem(g, NS)

                @pl.when((q == 0) & (s >= 2))
                def _():
                    fetch(g + NS - 2)

                fetch(g + NS - 1)
                with jax.named_scope("w_wg"):
                    gu_copy(wg_ref, q, slot, 0).wait()
                    gu_copy(wu_ref, q, slot, 1).wait()

                @pl.when(kc == 0)
                def _():
                    with jax.named_scope("gu"):
                        acc[n] = jnp.dot(xb[kc], ring[slot], preferred_element_type=F32)

                @pl.when((kc > 0) & (kc < NP - 1))
                def _():
                    with jax.named_scope("gu"):
                        acc[n] += jnp.dot(xb[kc], ring[slot], preferred_element_type=F32)

                @pl.when(kc == NP - 1)
                def _():
                    with jax.named_scope("gu"):
                        t = acc[n] + jnp.dot(xb[kc], ring[slot], preferred_element_type=F32)
                        hid[(s + 3) // 4, :, pl.ds(pl.multiple_of(n * GW, GW), GW)] = (
                            jax.nn.silu(t[:, :GW]) * t[:, GW:]).astype(BF16)

                @pl.when(s == 0)
                def _():
                    @pl.when((q == 9) | (q == 18))
                    def _():
                        relay_first(q // 18)

                    @pl.when((q == 11) | (q == 19))
                    def _():
                        partner_first(q // 18)

                @pl.when((s == 1) & ((q == 3) | (q == 10)))
                def _():
                    relay_first(2 + q // 10)

                @pl.when((s == 1) & ((q == 5) | (q == 12)))
                def _():
                    partner_first(2 + q // 10)

                @pl.when(s >= 2)
                def _():
                    @pl.when((q == 3) | (q == 11))
                    def _():
                        relay_end(s, 2 + q // 10)

                    @pl.when((q == 5) | (q == 13))
                    def _():
                        partner_end(s, 2 + q // 10)

                    @pl.when((s == 2) & ((q == 3) | (q == 14)))
                    def _():
                        relay_mid(2 + q // 10)

                    @pl.when(is_mid & (s == 3))
                    def _():
                        m = q % 7

                        @pl.when((m == 1) | (m == 3) | (m == 6))
                        def _():
                            pass_on(2 + 3 * (q // 7) + m // 3)

                        @pl.when((m == 0) | (m == 2) | (m == 5))
                        def _():
                            take(2 + 3 * (q // 7) + (m + 1) // 3)

        @pl.when(s > 0)
        def _():
            @pl.when((s == 1) | (s == 2))
            def _():
                load_mid(2 * s - 2 + s // 2)

            @pl.when(is_mid & (s == 3))
            def _():
                pass_on(jnp.int32(10))

            @pl.loop(0, ND2)
            def _(j):
                g = base + GU * (1 - s // 4) + 2 * j
                s0, s1 = lax.rem(g, NS), lax.rem(g + 1, NS)

                @pl.when((j > 0) | (s == 4))
                def _():
                    fetch(g + NS - 2)

                fetch(g + NS - 1)
                with jax.named_scope("w_wd"):
                    d_copy(2 * j, s0).wait()
                    d_copy(2 * j + 1, s1).wait()

                @pl.when(j >= 2)
                def _():
                    for h in range(2):
                        send_pt(s, 2 * j - PS + h).wait_send()

                hs = 1 - s // 4
                for h in range(2):
                    with jax.named_scope("d"):
                        cols = slice(h * DW, (h + 1) * DW)
                        t = jnp.dot(hid[hs, :, :FH], ring[s0, :FH, cols],
                                    preferred_element_type=F32)
                        t += jnp.dot(hid[hs, :, FH:], ring[s1, :FH, cols],
                                     preferred_element_type=F32)
                        stash[s % 4, 2 * j + h] = t[:R]
                        pst[(ND * (s - 1) + 2 * j + h) % PS] = t[R:].astype(BF16)

                def for_middle(do):
                    @pl.when((s == 2) & (j >= 5))
                    def _():
                        do(j - 5)

                    @pl.when((s == 3) & (j != 3) & (j < 6))
                    def _():
                        do(11 + j - j // 4)

                    @pl.when((s == 4) & (j % 3 != 2))
                    def _():
                        do(16 + j - (j + 1) // 3)

                def for_outer(do):
                    @pl.when(is_mid & (s == 4) & (j % 3 != 0))
                    def _():
                        do(j - 1 - j // 3)

                @pl.when(is_mid)
                def _():
                    for_middle(take)

                for_outer(lambda k: add_in(0, 2, k))

                @pl.when(j >= 1)
                def _():
                    fold(s, 2 * j - 2)
                    fold(s, 2 * j - 1)

                for h in range(2):
                    send_pt(s, 2 * j + h).start()

                @pl.when(j >= 1)
                def _():
                    end_send(s, 2 * j - 2)
                    end_send(s, 2 * j - 1)

                @pl.when(is_mid)
                def _():
                    for_middle(pass_on)

                for_outer(lambda k: send_rs(0, 0, k, outward).start())

                @pl.when((s == 1) | (s == 2))
                def _():
                    @pl.when((j == 0) | (j == 4))
                    def _():
                        relay_end(s + 1, j // 4)

                    @pl.when((j == 1) | (j == 5))
                    def _():
                        partner_end(s + 1, j // 4)

                    @pl.when((s == 1) & ((j == 0) | (j == 4)))
                    def _():
                        relay_mid(j // 4)

            fold(s, ND - 2)
            fold(s, ND - 1)

            @pl.loop(ND - PS, ND)
            def _(k):
                send_pt(s, k).wait_send()

            end_send(s, ND - 2)
            end_send(s, ND - 1)

    def y_copy(slot, k):
        return pltpu.make_async_copy(
            rs.at[slot, k], y_ref.at[:, pl.ds(pl.multiple_of(k * DW, DW), DW)], ysem.at[k])

    @pl.when(is_mid)
    def _():
        def finish(k):
            rs_arrived(1, k)
            rs_arrived(4, k)
            rs[1, k] = (stash[0, k] + rs[1, k].astype(F32) + rs[4, k].astype(F32)).astype(BF16)

        @pl.loop(0, ND - 4)
        def _(i):
            add_in(0, 2, 4 + i)

            @pl.when(i < ND2)
            def _():
                finish(2 * i)

            send_rs(0, 0, 4 + i, outward).start()

            @pl.when(i < ND2)
            def _():
                add_in(3, 3, 7 + i)
                finish(2 * i + 1)
                send_rs(3, 0, 7 + i, inward).start()
                y_copy(1, 2 * i).start()

            @pl.when((i > 0) & (i <= ND2))
            def _():
                y_copy(1, 2 * i - 1).start()

        @pl.loop(0, ND)
        def _(k):
            y_copy(1, k).wait()
            send_rs(2, 4, k, inward).wait_send()
            send_rs(3, 0, k, inward).wait_send()
            send_rs(0, 0, k, outward).wait_send()

    @pl.when(is_end)
    def _():
        @pl.loop(0, ND)
        def _(k):
            add_in(0, 0, k)

            @pl.when(k >= 1)
            def _():
                y_copy(0, k - 1).start()

        y_copy(0, ND - 1).start()

        @pl.loop(0, ND)
        def _(k):
            y_copy(0, k).wait()
            for s in (1, 2, 3):
                send_rs(s, s, k, inward).wait_send()

    @pl.loop(0, NP)
    def _(p):
        own_x(p, 0).wait_send()
        own_x(p, 1).wait_send()

        @pl.when(is_mid)
        def _():
            own_x(p, 2).wait_send()
            for bb in (0, 2, 3):
                forward(real(bb), p, inward).wait_send()
                share(real(bb), p).wait_send()

        @pl.when(is_end)
        def _():
            for bb in (1, 2, 3):
                share(real(bb), p).wait_send()


def solution(mesh):
    dma = pltpu.SemaphoreType.DMA

    def step(x, w_gate, w_up, w_down):
        hbm = pl.BlockSpec(memory_space=pltpu.HBM)
        y, _ = pl.pallas_call(
            kernel,
            name="mlp",
            out_shape=(jax.ShapeDtypeStruct((R, D), BF16),
                       jax.ShapeDtypeStruct((4, 2, NP, R, KC), BF16)),
            in_specs=[hbm] * 4,
            out_specs=(hbm, hbm),
            scratch_shapes=[
                pltpu.VMEM((NP, 2 * R, KC), BF16),
                pltpu.VMEM((NS, KC, 2 * GW), BF16),
                pltpu.VMEM((2, 2 * R, F), BF16),
                pltpu.VMEM((NG, 2 * R, 2 * GW), F32),
                pltpu.VMEM((4, ND, R, DW), F32),
                pltpu.VMEM((PS, R, DW), BF16),
                pltpu.VMEM((PS, R, DW), BF16),
                pltpu.VMEM((5, ND, R, DW), BF16),
                dma((NS, 2)), dma((2, NP)),
                dma((4, NP)), dma((4, NP)), dma((4, NP)), dma((4, NP)), dma((4, NP)),
                dma((PS,)), dma((PS,)), dma((4, ND)), dma((5, ND)), dma((ND,)),
            ],
            compiler_params=pltpu.CompilerParams(
                collective_id=0, has_side_effects=True, vmem_limit_bytes=67043328),
        )(x, w_gate, w_up, w_down)
        return y

    return jax.shard_map(
        step,
        mesh=mesh,
        in_specs=(P(("dp", "tp"), None), P(None, "tp"), P(None, "tp"), P("tp", None)),
        out_specs=P(("dp", "tp"), None),
        check_vma=False,
    )
```

time: 535 us -> 248 us (0.46)
  waiting for transfers between devices: 351 us -> 0 us
  Pallas kernels: 0 us -> 245 us
  matrix products: 171 us -> 0 us
  between operations: 13.4 us -> 0.01 us
    pallas_call x0 -> x1, Pallas kernels: none -> 245 us  [step(): pl.pallas_call(kernel, name='mlp', out_shape=(jax.ShapeDtypeStruct((R, D)...]
    reduce_scatter x1 -> x0, waiting for transfers between devices: 182 us -> none  [step(): return lax.psum_scatter(term, 'tp', scatter_dimension=0, tiled=True)]
    dot_general x3 -> x0, matrix products: 171 us -> none  [the longest x1 59.5 us: step(): up = jnp.dot(rows, w_up, preferred_element_type=jnp.float32)]
    all_gather x1 -> x0, waiting for transfers between devices: 168 us -> none  [step(): rows = lax.all_gather(x, 'tp', axis=0, tiled=True)]
  transfers between devices with their start and end apart: 2 -> 0, of which waited for: 2 -> 0; matrix products, arithmetic and copies ran while one was open for 0% -> 0% of each run, Pallas kernels for 0% -> 0%
where the time goes in v2:
time: 248 us
  Pallas kernels  245 us (99%)
  local copies, waits for them, and re-layouts  3.18 us (1%)
    pallas_call x1, Pallas kernels, step(): pl.pallas_call(kernel, name='mlp', out_shape=(jax.ShapeDtypeStruct((R, D)...  245 us

profile of v2, /device:TPU:0, one launch (start us, length us, event | category | flops | bytes accessed | tf_op | source)
XLA Modules:
  0.0 247.8 jit_solution(3932690342863136718)
XLA Ops:
  0.0 244.6 %mlp.1 = (bf16[160,7168]{1,0:T(8,128)(2,1)}, bf16[4,2,4,160,1792]{4,3,2,1,0:T(8,128)(2,1)}) custom-call(bf16[160,7168]{1,0:T(8,128)(2,1)} %x_ref.1, bf16[7168,2560]{1,0:T(8,128)(2,1)} %wg_ref.1, bf16[7168,2560]{1,0:T(8,128)(2,1)} %wu_ref.1, bf16[2560,7168]{1,0:T(8,128)(2,1)} %wd_ref.1), custom_call_target="tpu_custom_call" | custom-call | tf_op jit(solution)/shard_map/mlp/pallas_call | solution.py:532
  244.6 3.2 %copy.6 = bf16[160,7168]{1,0:T(8,128)(2,1)} copy(bf16[160,7168]{1,0:T(8,128)(2,1)} %get-tuple-element.6) | data formatting | bytes 4587520

commit v3 on v2

v3 whole, which is shorter than its diff:
```python
import functools

import jax
import jax.numpy as jnp
from jax import lax
from jax.experimental import pallas as pl
from jax.experimental.pallas import tpu as pltpu
from jax.sharding import PartitionSpec as P

MESH = pl.DeviceIdType.MESH
F32, BF16 = jnp.float32, jnp.bfloat16

D = 7168
F = 2560
R = 160
NP = 4
KC = D // NP
GW, NG = 512, F // 512
DW, ND = 512, D // 512
ND2, FH = ND // 2, F // 2
GU = NP * NG
NS = 5
TAKES = (0, 2, 4, 6, 8, 11, 13, 15, 18)
PS = 4


def kernel(x_ref, wg_ref, wu_ref, wd_ref, y_ref, xg, xb, ring, hid, acc, stash, pst, pt, rs,
           wsem, xsem, ag_recv, agp_recv, fwd_send, out_send, d2d_send,
           pst_send, pt_recv, rs_send, rs_recv, ysem):
    tp = lax.axis_index("tp")
    z, c = tp // 2, tp % 2
    mir = z // 2
    mid = (z * (3 - z)) // 2
    is_mid, is_end = mid == 1, mid == 0
    din = 1 - 2 * mir
    partner = {"tp": 2 * z + (1 - c)}
    inward = {"tp": 2 * (z + din) + c}
    outward = {"tp": 2 * (z - din * mid) + c}

    def real(bb):
        return bb + mir * (3 - 2 * bb)

    barrier = pltpu.get_barrier_semaphore()
    pl.semaphore_signal(barrier, inc=1, device_id=partner, device_id_type=MESH)
    pl.semaphore_signal(barrier, inc=1, device_id=inward, device_id_type=MESH)

    @pl.when(is_mid)
    def _():
        pl.semaphore_signal(barrier, inc=1, device_id=outward, device_id_type=MESH)

    def gu_copy(ref, u, slot, h):
        return pltpu.make_async_copy(
            ref.at[pl.ds(pl.multiple_of((u // NG) * KC, KC), KC),
                   pl.ds(pl.multiple_of((u % NG) * GW, GW), GW)],
            ring.at[slot, :, pl.ds(h * GW, GW)], wsem.at[slot, h])

    def fetch_gu(u, slot):
        gu_copy(wg_ref, u, slot, 0).start()
        gu_copy(wu_ref, u, slot, 1).start()

    def d_copy(d, slot):
        return pltpu.make_async_copy(
            wd_ref.at[pl.ds(pl.multiple_of((d % 2) * FH, FH), FH),
                      pl.ds(pl.multiple_of((d // 2) * 2 * DW, 2 * DW), 2 * DW)],
            ring.at[slot, pl.ds(0, FH)], wsem.at[slot, 0])

    def fetch_d(d):
        d_copy(d, lax.rem(d, NS)).start()

    for u in range(NS - 1):
        fetch_gu(u, u)

    def send_x(src, b, p, sem, recv, dev):
        return pltpu.make_async_remote_copy(
            src_ref=src, dst_ref=xg.at[b, c, p], send_sem=sem.at[b, p],
            recv_sem=recv.at[b, p], device_id=dev, device_id_type=MESH)

    def own_cols(p):
        return x_ref.at[:, pl.ds(pl.multiple_of(p * KC, KC), KC)]

    def own_x(p, kind):
        if kind == 0:
            return send_x(own_cols(p), z, p, d2d_send, agp_recv, partner)
        if kind == 1:
            return send_x(own_cols(p), z, p, fwd_send, ag_recv, inward)
        return send_x(own_cols(p), z, p, out_send, ag_recv, outward)

    def arrived(b, p):
        with jax.named_scope("w_ag"):
            send_x(xg.at[b, c, p], b, p, fwd_send, ag_recv, partner).wait_recv()

    def forward(b, p, dev):
        return send_x(xg.at[b, c, p], b, p, fwd_send, ag_recv, dev)

    def share(b, p):
        return send_x(xg.at[b, c, p], b, p, d2d_send, agp_recv, partner)

    def load_own(b, p):
        return pltpu.make_async_copy(xg.at[b, c, p], xb.at[p, pl.ds(0, R)], xsem.at[0, p])

    def load_partner(b, p):
        return pltpu.make_async_copy(xg.at[b, 1 - c, p], xb.at[p, pl.ds(R, R)], xsem.at[1, p])

    def partner_piece(b, p):
        with jax.named_scope("w_px"):
            pltpu.make_async_remote_copy(
                src_ref=xg.at[b, 1 - c, p], dst_ref=xg.at[b, 1 - c, p],
                send_sem=d2d_send.at[b, p], recv_sem=agp_recv.at[b, p],
                device_id=partner, device_id_type=MESH).wait_recv()
        load_partner(b, p).start()

    def relay_first(p):
        b = real(1 - mid)
        arrived(b, p)

        @pl.when(is_mid)
        def _():
            forward(b, p, inward).start()

        share(b, p).start()
        load_own(b, p).start()

    def partner_first(p):
        partner_piece(real(1 - mid), p)

    def relay_end(s, p):
        arrived(real(5 - s), p)
        share(real(5 - s), p).start()
        load_own(real(5 - s), p).start()

    def partner_end(s, p):
        partner_piece(real(5 - s), p)

    def relay_mid(bb, p):
        arrived(real(bb), p)
        forward(real(bb), p, outward).start()
        share(real(bb), p).start()

    def load_mid(bb):
        @pl.loop(0, NP)
        def _(p):
            load_own(real(bb), p).start()
            partner_piece(real(bb), p)

    def send_pt(s, j):
        k = (ND * (s - 1) + j) % PS
        return pltpu.make_async_remote_copy(
            src_ref=pst.at[k], dst_ref=pt.at[k], send_sem=pst_send.at[k],
            recv_sem=pt_recv.at[k], device_id=partner, device_id_type=MESH)

    def send_rs(slot, there, j, dev):
        return pltpu.make_async_remote_copy(
            src_ref=rs.at[slot, j], dst_ref=rs.at[there, j], send_sem=rs_send.at[slot, j],
            recv_sem=rs_recv.at[there, j], device_id=dev, device_id_type=MESH)

    def rs_arrived(slot, j):
        with jax.named_scope(f"w_rs{slot}"):
            send_rs(0, slot, j, inward).wait_recv()

    def fold(s, k):
        with jax.named_scope("w_pt"):
            send_pt(s, k).wait_recv()
        v = stash[s % 4, k] + pt[(ND * (s - 1) + k) % PS].astype(F32)

        @pl.when(is_end & (s < 4))
        def _():
            rs[s, k] = v.astype(BF16)

        @pl.when(is_mid | (s == 4))
        def _():
            stash[s % 4, k] = v

    def end_send(s, k):
        @pl.when(is_end & (s < 4))
        def _():
            send_rs(s, s, k, inward).start()

    def add_in(slot, s, k):
        rs_arrived(slot, k)
        rs[slot, k] = (stash[s, k] + rs[slot, k].astype(F32)).astype(BF16)

    def pass_on(k):
        @pl.when(k < ND)
        def _():
            send_rs(2, 0, k, inward).start()

        @pl.when(k >= ND)
        def _():
            send_rs(3, 4, k - ND, inward).start()

    def take(k):
        @pl.when(k < ND)
        def _():
            add_in(2, 2, k)

        @pl.when(k >= ND)
        def _():
            add_in(3, 3, k - ND)

    def x_own(p):
        return pltpu.make_async_copy(own_cols(p), xb.at[p, pl.ds(0, R)], xsem.at[0, p])

    for p in range(NP):
        x_own(p).start()
    with jax.named_scope("w_bar"):
        pl.semaphore_wait(barrier, 2 + mid)

    @pl.loop(0, NP)
    def _(p):
        own_x(p, 0).start()

        @pl.when(is_end | (p == 0))
        def _():
            own_x(p, 1).start()

        @pl.when(is_mid)
        def _():
            own_x(p, 2).start()

    partner_piece(z, 0)

    def gu_events(s, kc, n):
        def at(when, q, fn):
            if q // NG == kc:
                @pl.when(when & (n == q % NG))
                def _():
                    fn()

        first, second, both = s == 0, s == 1, (s == 2) | (s == 3)
        for p in range(1, NP):
            at(first, p - 1, functools.partial(partner_piece, z, p))
        at(first, 9, lambda: relay_first(0))
        at(first, 11, lambda: partner_first(0))
        at(first, 18, lambda: relay_first(1))
        at(first, 19, lambda: partner_first(1))
        at(first & is_mid, 19, lambda: relay_mid(3, 0))
        at(second, 5, lambda: relay_first(2))
        at(second, 7, lambda: partner_first(2))
        at(second & is_mid, 10, lambda: relay_mid(3, 1))
        at(second, 12, lambda: relay_first(3))

        def own_rest():
            for p in range(1, NP):
                own_x(p, 1).start()

        at(second & is_mid, 12, own_rest)
        at(second, 14, lambda: partner_first(3))
        at(second & is_mid, 18, lambda: relay_mid(3, 2))
        for i, q in enumerate((0, 7, 15)):
            at((s == 2) & is_mid, q, functools.partial(relay_mid, 2, 1 + i))
        at(both & is_end, 1, lambda: partner_end(s, 1))
        at(both & is_end, 6, lambda: relay_end(s, 2))
        at(both & is_end, 8, lambda: partner_end(s, 2))
        at(both & is_end, 12, lambda: relay_end(s, 3))
        at(both & is_end, 14, lambda: partner_end(s, 3))
        for i, q in enumerate(TAKES):
            at((s == 3) & is_mid, q, functools.partial(take, jnp.int32(3 + i)))

    def gu_sends(s, kc, n):
        for i, q in enumerate(TAKES):
            if (q + 1) // NG == kc:
                @pl.when((s == 3) & is_mid & (n == (q + 1) % NG))
                def _():
                    pass_on(jnp.int32(3 + i))

    @pl.loop(0, 5)
    def _(s):
        @pl.when(s < 4)
        def _():
            @pl.when(s >= 2)
            def _():
                fetch_gu(2, 2)
                fetch_gu(3, 3)

            for kc in range(NP):
                with jax.named_scope("w_xl"):
                    load_own(z, kc).wait()
                    load_partner(z, kc).wait()

                @pl.loop(0, NG)
                def _(n):
                    if kc < NP - 1:
                        fetch_gu(kc * NG + n + NS - 1, (n + NS - 1) % NS)
                    else:
                        @pl.when(n == 0)
                        def _():
                            fetch_gu(GU - 1, NS - 1)

                        @pl.when((n > 0) & (s == 0))
                        def _():
                            fetch_gu(n - 1, n - 1)

                        @pl.when((n > 0) & (s > 0))
                        def _():
                            fetch_d(n - 1)

                    gu_sends(s, kc, n)
                    with jax.named_scope("w_wg"):
                        gu_copy(wg_ref, kc * NG + n, n, 0).wait()
                        gu_copy(wu_ref, kc * NG + n, n, 1).wait()
                    with jax.named_scope("gu"):
                        t = jnp.dot(xb[kc], ring[n], preferred_element_type=F32)
                        if kc == 0:
                            acc[n] = t
                        elif kc < NP - 1:
                            acc[n] += t
                        else:
                            t += acc[n]
                            hid[(s + 3) // 4, :, pl.ds(pl.multiple_of(n * GW, GW), GW)] = (
                                jax.nn.silu(t[:, :GW]) * t[:, GW:]).astype(BF16)
                    gu_events(s, kc, n)

        @pl.when(s > 0)
        def _():
            @pl.when(is_mid & (s >= 3))
            def _():
                take(12 + 5 * (s - 3))

            @pl.loop(0, ND2)
            def _(j):
                s0, s1 = lax.rem(2 * j, NS), lax.rem(2 * j + 1, NS)

                @pl.when(j == 0)
                def _():
                    @pl.when(s == 4)
                    def _():
                        fetch_d(jnp.int32(2))
                        fetch_d(jnp.int32(3))

                    fetch_d(jnp.int32(4))

                @pl.when((j > 0) & (j < 6))
                def _():
                    fetch_d(2 * j + 3)

                @pl.when((j > 0) & (j < 5))
                def _():
                    fetch_d(2 * j + 4)

                @pl.when((j == 6) & (s < 3))
                def _():
                    fetch_gu(0, 0)
                    fetch_gu(1, 1)

                @pl.when((j == 6) & (s == 3))
                def _():
                    fetch_d(jnp.int32(0))
                    fetch_d(jnp.int32(1))

                @pl.when(is_mid & (s >= 3) & (j == 0))
                def _():
                    pass_on(12 + 5 * (s - 3))

                with jax.named_scope("w_wd"):
                    d_copy(2 * j, s0).wait()
                    d_copy(2 * j + 1, s1).wait()

                @pl.when(j >= 2)
                def _():
                    for h in range(2):
                        send_pt(s, 2 * j - PS + h).wait_send()

                hs = 1 - s // 4
                for h in range(2):
                    with jax.named_scope("d"):
                        cols = slice(h * DW, (h + 1) * DW)
                        t = jnp.dot(hid[hs, :, :FH], ring[s0, :FH, cols],
                                    preferred_element_type=F32)
                        t += jnp.dot(hid[hs, :, FH:], ring[s1, :FH, cols],
                                     preferred_element_type=F32)
                        stash[s % 4, 2 * j + h] = t[:R]
                        pst[(ND * (s - 1) + 2 * j + h) % PS] = t[R:].astype(BF16)

                def for_middle(do):
                    @pl.when((s == 2) & (j >= 3) & (j < 6))
                    def _():
                        do(j - 3)

                    @pl.when((s == 3) & (j % 3 != 2) & (j > 0))
                    def _():
                        do(12 + j - j // 3)

                    @pl.when((s == 4) & (j % 3 != 0))
                    def _():
                        do(17 + j - j // 3)

                def for_outer(do):
                    @pl.when(is_mid & (s >= 3))
                    def _():
                        do((s - 3) * ND2 + j)

                @pl.when(is_mid)
                def _():
                    for_middle(take)

                for_outer(lambda k: add_in(0, 1, k))

                @pl.when(j >= 1)
                def _():
                    fold(s, 2 * j - 2)
                    fold(s, 2 * j - 1)

                for h in range(2):
                    send_pt(s, 2 * j + h).start()

                @pl.when(j >= 1)
                def _():
                    end_send(s, 2 * j - 2)
                    end_send(s, 2 * j - 1)

                @pl.when(is_mid)
                def _():
                    for_middle(pass_on)

                for_outer(lambda k: send_rs(0, 0, k, outward).start())

                @pl.when((s == 1) | (s == 2))
                def _():
                    @pl.when(is_end & ((j == 0) | (j == 6)))
                    def _():
                        relay_end(s + 1, j // 6)

                    @pl.when(is_end & (j == 1))
                    def _():
                        partner_end(s + 1, 0)

                    @pl.when(is_mid & (s == 1) & (j == 3))
                    def _():
                        relay_mid(3, 3)
                        relay_mid(2, 0)

                    @pl.when(is_mid & (j == 5))
                    def _():
                        load_mid(4 - s)

            fold(s, ND - 2)
            fold(s, ND - 1)

            @pl.loop(ND - PS, ND)
            def _(k):
                send_pt(s, k).wait_send()

            end_send(s, ND - 2)
            end_send(s, ND - 1)

    def y_copy(slot, k):
        return pltpu.make_async_copy(
            rs.at[slot, k], y_ref.at[:, pl.ds(pl.multiple_of(k * DW, DW), DW)], ysem.at[k])

    @pl.when(is_mid)
    def _():
        def finish(k):
            rs_arrived(1, k)
            rs_arrived(4, k)
            rs[1, k] = (stash[0, k] + rs[1, k].astype(F32) + rs[4, k].astype(F32)).astype(BF16)

        @pl.loop(0, ND2)
        def _(i):
            @pl.when(i < ND2 - 1)
            def _():
                add_in(3, 3, 8 + i)

            finish(2 * i)

            @pl.when(i < ND2 - 1)
            def _():
                send_rs(3, 4, 8 + i, inward).start()

            @pl.when(i > 0)
            def _():
                y_copy(1, 2 * i - 1).start()

            finish(2 * i + 1)
            y_copy(1, 2 * i).start()

        y_copy(1, ND - 1).start()

        @pl.loop(0, ND)
        def _(k):
            y_copy(1, k).wait()
            send_rs(2, 0, k, inward).wait_send()
            send_rs(3, 4, k, inward).wait_send()
            send_rs(0, 0, k, outward).wait_send()

    @pl.when(is_end)
    def _():
        @pl.loop(0, ND)
        def _(k):
            add_in(0, 0, k)

            @pl.when(k >= 1)
            def _():
                y_copy(0, k - 1).start()

        y_copy(0, ND - 1).start()

        @pl.loop(0, ND)
        def _(k):
            y_copy(0, k).wait()
            for s in (1, 2, 3):
                send_rs(s, s, k, inward).wait_send()

    @pl.loop(0, NP)
    def _(p):
        own_x(p, 0).wait_send()
        own_x(p, 1).wait_send()

        @pl.when(is_mid)
        def _():
            own_x(p, 2).wait_send()
            for bb in (0, 2, 3):
                forward(real(bb), p, inward).wait_send()
                share(real(bb), p).wait_send()

        @pl.when(is_end)
        def _():
            for bb in (1, 2, 3):
                share(real(bb), p).wait_send()


def solution(mesh):
    dma = pltpu.SemaphoreType.DMA

    def step(x, w_gate, w_up, w_down):
        hbm = pl.BlockSpec(memory_space=pltpu.HBM)
        y, _ = pl.pallas_call(
            kernel,
            name="mlp",
            out_shape=(jax.ShapeDtypeStruct((R, D), BF16),
                       jax.ShapeDtypeStruct((4, 2, NP, R, KC), BF16)),
            in_specs=[hbm] * 4,
            out_specs=(hbm, hbm),
            scratch_shapes=[
                pltpu.VMEM((NP, 2 * R, KC), BF16),
                pltpu.VMEM((NS, KC, 2 * GW), BF16),
                pltpu.VMEM((2, 2 * R, F), BF16),
                pltpu.VMEM((NG, 2 * R, 2 * GW), F32),
                pltpu.VMEM((4, ND, R, DW), F32),
                pltpu.VMEM((PS, R, DW), BF16),
                pltpu.VMEM((PS, R, DW), BF16),
                pltpu.VMEM((5, ND, R, DW), BF16),
                dma((NS, 2)), dma((2, NP)),
                dma((4, NP)), dma((4, NP)), dma((4, NP)), dma((4, NP)), dma((4, NP)),
                dma((PS,)), dma((PS,)), dma((4, ND)), dma((5, ND)), dma((ND,)),
            ],
            compiler_params=pltpu.CompilerParams(
                collective_id=0, has_side_effects=True, vmem_limit_bytes=67043328),
        )(x, w_gate, w_up, w_down)
        return y

    return jax.shard_map(
        step,
        mesh=mesh,
        in_specs=(P(("dp", "tp"), None), P(None, "tp"), P(None, "tp"), P("tp", None)),
        out_specs=P(("dp", "tp"), None),
        check_vma=False,
    )
```

time: 248 us -> 236 us (0.952)
  the two profiles are of different devices: /device:TPU:0 before, /device:TPU:15 now
where the time goes in v3:
time: 236 us
  Pallas kernels  233 us (99%)
  local copies, waits for them, and re-layouts  3.18 us (1%)
    pallas_call x1, Pallas kernels, step(): pl.pallas_call(kernel, name='mlp', out_shape=(jax.ShapeDtypeStruct((R, D)...  233 us

profile of v3, /device:TPU:15, one launch (start us, length us, event | category | flops | bytes accessed | tf_op | source)
XLA Modules:
  0.0 236.0 jit_solution(8519354190610151336)
XLA Ops:
  0.0 232.8 %mlp.1 = (bf16[160,7168]{1,0:T(8,128)(2,1)}, bf16[4,2,4,160,1792]{4,3,2,1,0:T(8,128)(2,1)}) custom-call(bf16[160,7168]{1,0:T(8,128)(2,1)} %x_ref.1, bf16[7168,2560]{1,0:T(8,128)(2,1)} %wg_ref.1, bf16[7168,2560]{1,0:T(8,128)(2,1)} %wu_ref.1, bf16[2560,7168]{1,0:T(8,128)(2,1)} %wd_ref.1), custom_call_target="tpu_custom_call" | custom-call | tf_op jit(solution)/shard_map/mlp/pallas_call | solution.py:526
  232.8 3.2 %copy.6 = bf16[160,7168]{1,0:T(8,128)(2,1)} copy(bf16[160,7168]{1,0:T(8,128)(2,1)} %get-tuple-element.6) | data formatting | bytes 4587520

commit v4 on v3

--- a/solution.py
+++ b/solution.py
@@ -26,7 +26,7 @@
 
 def kernel(x_ref, wg_ref, wu_ref, wd_ref, y_ref, xg, xb, ring, hid, acc, stash, pst, pt, rs,
            wsem, xsem, ag_recv, agp_recv, fwd_send, out_send, d2d_send,
-           pst_send, pt_recv, rs_send, rs_recv, ysem):
+           pst_send, pt_recv, rs_send, rs_recv):
     tp = lax.axis_index("tp")
     z, c = tp // 2, tp % 2
     mir = z // 2
@@ -148,10 +148,20 @@
             src_ref=pst.at[k], dst_ref=pt.at[k], send_sem=pst_send.at[k],
             recv_sem=pt_recv.at[k], device_id=partner, device_id_type=MESH)
 
+    def cols_of(k):
+        return pl.ds(pl.multiple_of(k * DW, DW), DW)
+
     def send_rs(slot, there, j, dev):
+        sem = 4 if isinstance(there, int) and there == 1 else there
         return pltpu.make_async_remote_copy(
             src_ref=rs.at[slot, j], dst_ref=rs.at[there, j], send_sem=rs_send.at[slot, j],
-            recv_sem=rs_recv.at[there, j], device_id=dev, device_id_type=MESH)
+            recv_sem=rs_recv.at[sem, j], device_id=dev, device_id_type=MESH)
+
+    def send_first(j):
+        return pltpu.make_async_remote_copy(
+            src_ref=y_ref.at[:, cols_of(j)], dst_ref=y_ref.at[:, cols_of(j)],
+            send_sem=rs_send.at[1, j], recv_sem=rs_recv.at[1, j],
+            device_id=inward, device_id_type=MESH)
 
     def rs_arrived(slot, j):
         with jax.named_scope(f"w_rs{slot}"):
@@ -162,7 +172,11 @@
             send_pt(s, k).wait_recv()
         v = stash[s % 4, k] + pt[(ND * (s - 1) + k) % PS].astype(F32)
 
-        @pl.when(is_end & (s < 4))
+        @pl.when(is_end & (s == 1))
+        def _():
+            y_ref[:, cols_of(k)] = v.astype(BF16)
+
+        @pl.when(is_end & (s > 1) & (s < 4))
         def _():
             rs[s, k] = v.astype(BF16)
 
@@ -171,7 +185,11 @@
             stash[s % 4, k] = v
 
     def end_send(s, k):
-        @pl.when(is_end & (s < 4))
+        @pl.when(is_end & (s == 1))
+        def _():
+            send_first(k).start()
+
+        @pl.when(is_end & (s > 1) & (s < 4))
         def _():
             send_rs(s, s, k, inward).start()
 
@@ -186,7 +204,7 @@
 
         @pl.when(k >= ND)
         def _():
-            send_rs(3, 4, k - ND, inward).start()
+            send_rs(3, 1, k - ND, inward).start()
 
     def take(k):
         @pl.when(k < ND)
@@ -244,7 +262,7 @@
                 own_x(p, 1).start()
 
         at(second & is_mid, 12, own_rest)
-        at(second, 14, lambda: partner_first(3))
+        at(second, 13, lambda: partner_first(3))
         at(second & is_mid, 18, lambda: relay_mid(3, 2))
         for i, q in enumerate((0, 7, 15)):
             at((s == 2) & is_mid, q, functools.partial(relay_mid, 2, 1 + i))
@@ -252,7 +270,7 @@
         at(both & is_end, 6, lambda: relay_end(s, 2))
         at(both & is_end, 8, lambda: partner_end(s, 2))
         at(both & is_end, 12, lambda: relay_end(s, 3))
-        at(both & is_end, 14, lambda: partner_end(s, 3))
+        at(both & is_end, 13, lambda: partner_end(s, 3))
         for i, q in enumerate(TAKES):
             at((s == 3) & is_mid, q, functools.partial(take, jnp.int32(3 + i)))
 
@@ -443,16 +461,35 @@
             end_send(s, ND - 2)
             end_send(s, ND - 1)
 
-    def y_copy(slot, k):
-        return pltpu.make_async_copy(
-            rs.at[slot, k], y_ref.at[:, pl.ds(pl.multiple_of(k * DW, DW), DW)], ysem.at[k])
+    @pl.loop(0, NP)
+    def _(p):
+        own_x(p, 0).wait_send()
+        own_x(p, 1).wait_send()
+
+        @pl.when(is_mid)
+        def _():
+            own_x(p, 2).wait_send()
+            for bb in (0, 2, 3):
+                forward(real(bb), p, inward).wait_send()
+                share(real(bb), p).wait_send()
+
+        @pl.when(is_end)
+        def _():
+            for bb in (1, 2, 3):
+                share(real(bb), p).wait_send()
 
     @pl.when(is_mid)
     def _():
         def finish(k):
+            send_first(k).wait_recv()
             rs_arrived(1, k)
-            rs_arrived(4, k)
-            rs[1, k] = (stash[0, k] + rs[1, k].astype(F32) + rs[4, k].astype(F32)).astype(BF16)
+            y_ref[:, cols_of(k)] = (
+                stash[0, k] + y_ref[:, cols_of(k)].astype(F32) + rs[1, k].astype(F32)).astype(BF16)
+
+        def done(k):
+            send_rs(2, 0, k, inward).wait_send()
+            send_rs(0, 0, k, outward).wait_send()
+            send_rs(3, 1, k, inward).wait_send()
 
         @pl.loop(0, ND2)
         def _(i):
@@ -464,58 +501,27 @@
 
             @pl.when(i < ND2 - 1)
             def _():
-                send_rs(3, 4, 8 + i, inward).start()
+                send_rs(3, 1, 8 + i, inward).start()
+
+            finish(2 * i + 1)
 
             @pl.when(i > 0)
             def _():
-                y_copy(1, 2 * i - 1).start()
-
-            finish(2 * i + 1)
-            y_copy(1, 2 * i).start()
-
-        y_copy(1, ND - 1).start()
-
-        @pl.loop(0, ND)
-        def _(k):
-            y_copy(1, k).wait()
-            send_rs(2, 0, k, inward).wait_send()
-            send_rs(3, 4, k, inward).wait_send()
-            send_rs(0, 0, k, outward).wait_send()
+                done(2 * i - 2)
+                done(2 * i - 1)
+
+        done(ND - 2)
+        done(ND - 1)
 
     @pl.when(is_end)
     def _():
         @pl.loop(0, ND)
         def _(k):
-            add_in(0, 0, k)
-
-            @pl.when(k >= 1)
-            def _():
-                y_copy(0, k - 1).start()
-
-        y_copy(0, ND - 1).start()
-
-        @pl.loop(0, ND)
-        def _(k):
-            y_copy(0, k).wait()
-            for s in (1, 2, 3):
+            rs_arrived(0, k)
+            send_first(k).wait_send()
+            y_ref[:, cols_of(k)] = (stash[0, k] + rs[0, k].astype(F32)).astype(BF16)
+            for s in (2, 3):
                 send_rs(s, s, k, inward).wait_send()
-
-    @pl.loop(0, NP)
-    def _(p):
-        own_x(p, 0).wait_send()
-        own_x(p, 1).wait_send()
-
-        @pl.when(is_mid)
-        def _():
-            own_x(p, 2).wait_send()
-            for bb in (0, 2, 3):
-                forward(real(bb), p, inward).wait_send()
-                share(real(bb), p).wait_send()
-
-        @pl.when(is_end)
-        def _():
-            for bb in (1, 2, 3):
-                share(real(bb), p).wait_send()
 
 
 def solution(mesh):
@@ -526,10 +532,10 @@
         y, _ = pl.pallas_call(
             kernel,
             name="mlp",
-            out_shape=(jax.ShapeDtypeStruct((R, D), BF16),
+            out_shape=(pltpu.VMEM((R, D), BF16),
                        jax.ShapeDtypeStruct((4, 2, NP, R, KC), BF16)),
             in_specs=[hbm] * 4,
-            out_specs=(hbm, hbm),
+            out_specs=(pl.BlockSpec(memory_space=pltpu.VMEM), hbm),
             scratch_shapes=[
                 pltpu.VMEM((NP, 2 * R, KC), BF16),
                 pltpu.VMEM((NS, KC, 2 * GW), BF16),
@@ -538,13 +544,13 @@
                 pltpu.VMEM((4, ND, R, DW), F32),
                 pltpu.VMEM((PS, R, DW), BF16),
                 pltpu.VMEM((PS, R, DW), BF16),
-                pltpu.VMEM((5, ND, R, DW), BF16),
+                pltpu.VMEM((4, ND, R, DW), BF16),
                 dma((NS, 2)), dma((2, NP)),
                 dma((4, NP)), dma((4, NP)), dma((4, NP)), dma((4, NP)), dma((4, NP)),
-                dma((PS,)), dma((PS,)), dma((4, ND)), dma((5, ND)), dma((ND,)),
+                dma((PS,)), dma((PS,)), dma((4, ND)), dma((5, ND)),
             ],
             compiler_params=pltpu.CompilerParams(
-                collective_id=0, has_side_effects=True, vmem_limit_bytes=67043328),
+                collective_id=0, has_side_effects=True, vmem_limit_bytes=64600000),
         )(x, w_gate, w_up, w_down)
         return y
 

time: 236 us -> 232 us (0.983)
  the two profiles are of different devices: /device:TPU:15 before, /device:TPU:10 now
where the time goes in v4:
time: 232 us
  Pallas kernels  231 us (100%)
    pallas_call x1, Pallas kernels, step(): pl.pallas_call(kernel, name='mlp', out_shape=(pltpu.VMEM((R, D), BF16), j...  231 us

profile of v4, /device:TPU:10, one launch (start us, length us, event | category | flops | bytes accessed | tf_op | source)
XLA Modules:
  0.0 232.3 jit_solution(14857478961981705013)
XLA Ops:
  0.0 230.9 %mlp.1 = (bf16[160,7168]{1,0:T(8,128)(2,1)S(1)}, bf16[4,2,4,160,1792]{4,3,2,1,0:T(8,128)(2,1)}) custom-call(bf16[160,7168]{1,0:T(8,128)(2,1)} %x_ref.1, bf16[7168,2560]{1,0:T(8,128)(2,1)} %wg_ref.1, bf16[7168,2560]{1,0:T(8,128)(2,1)} %wu_ref.1, bf16[2560,7168]{1,0:T(8,128)(2,1)} %wd_ref.1), custom_call_target="tpu_custom_call" | custom-call | tf_op jit(solution)/shard_map/mlp/pallas_call | solution.py:532
  230.9 1.4 copy.6
